TPU v7x, 8 devices: a whole 2x2x1 slice. The times are simulated.
8 devices in a mesh: rep: 1 (over z), dp: 8 (over x, y, core).
Axes of the slice: x: 2, y: 2, z: 1, core: 2. Of those that a mesh axis runs over, the one named last changes fastest.
Arguments:
- x: bfloat16 [8, 2048, 1024], P(('rep', 'dp'))
- dy: bfloat16 [8, 2048, 1024], P(('rep', 'dp'))
- w_gate: bfloat16 [2, 1024, 4096], replicated
- w_up: bfloat16 [2, 1024, 4096], replicated
- w_down: bfloat16 [2, 4096, 1024], replicated
- m_w_gate: float32 [2, 1024, 4096], replicated
- m_w_up: float32 [2, 1024, 4096], replicated
- m_w_down: float32 [2, 4096, 1024], replicated
- v_w_gate: float32 [2, 1024, 4096], replicated
- v_w_up: float32 [2, 1024, 4096], replicated
- v_w_down: float32 [2, 4096, 1024], replicated
Outputs:
- output 1: bfloat16 [2, 1024, 4096], P('rep')
- output 2: bfloat16 [2, 1024, 4096], P('rep')
- output 3: bfloat16 [2, 4096, 1024], P('rep')
- output 4: float32 [2, 1024, 4096], P('rep')
- output 5: float32 [2, 1024, 4096], P('rep')
- output 6: float32 [2, 4096, 1024], P('rep')
- output 7: float32 [2, 1024, 4096], P('rep')
- output 8: float32 [2, 1024, 4096], P('rep')
- output 9: float32 [2, 4096, 1024], P('rep')
All inputs are finite; a program needn't handle non-finite values.
Results may differ from a plain program's by a relative error of at most 0.022.
Values are sent between devices in bfloat16 or wider.
A program may use at most 2.75 GiB of HBM per device.

v0:
```python
import jax
import jax.numpy as jnp
from jax import lax
from jax.sharding import PartitionSpec as P

NAMES = ("w_gate", "w_up", "w_down")


def matmul(a, w):
    return jnp.dot(a, w, preferred_element_type=jnp.float32).astype(jnp.bfloat16)


def normed(h):
    wide = h.astype(jnp.float32)
    scale = lax.rsqrt(jnp.mean(wide**2, -1, keepdims=True) + 1e-6)
    return (wide * scale).astype(jnp.bfloat16)


def layer(h, w):
    a = normed(h)
    gate = jnp.dot(a, w["w_gate"], preferred_element_type=jnp.float32)
    up = jnp.dot(a, w["w_up"], preferred_element_type=jnp.float32)
    return h + matmul((jax.nn.silu(gate) * up).astype(jnp.bfloat16), w["w_down"])


def adamw(w, m, v, g):
    m = 0.9 * m + 0.1 * g
    v = 0.95 * v + 0.05 * g * g
    step = m * lax.rsqrt(v + 1e-8) + 0.1 * w
    return (w - 0.02 * step).astype(jnp.bfloat16), m, v


def solution(mesh):
    def step(x, dy, *arrays):
        weights, m, v = (arrays[i : i + 3] for i in (0, 3, 6))
        layers = weights[0].shape[0]
        h, kept = x[0], []
        for number in range(layers):
            kept.append(h)
            h = layer(h, {name: w[number] for name, w in zip(NAMES, weights, strict=True)})
        by_h, summed = dy[0], [None] * layers
        for number in reversed(range(layers)):
            _, back = jax.vjp(lambda w, h: layer(h, w), {name: w[number] for name, w in zip(NAMES, weights, strict=True)}, kept[number])
            by_w, by_h = back(by_h)
            summed[number] = [lax.psum(by_w[name], "dp") for name in NAMES]
        gradients = [jnp.stack([summed[number][i] for number in range(layers)]).astype(jnp.float32) for i in range(3)]
        new = [adamw(w.astype(jnp.float32), m, v, g) for w, m, v, g in zip(weights, m, v, gradients, strict=True)]
        return tuple(one[which] for which in range(3) for one in new)

    return jax.shard_map(
        step,
        mesh=mesh,
        in_specs=(P(("rep", "dp"), None, None),) * 2 + (P(None, None, None),) * 9,
        out_specs=(P("rep", None, None),) * 9,
        check_vma=False,
    )
```

profile of v0, /device:TPU:0, one launch (start us, length us, event | category | flops | bytes accessed | tf_op | source)
XLA Modules:
  0.0 1206.9 jit_solution(14407604841569564425)
XLA Ops:
  7.2 6.5 copy.20
  13.8 3.1 fusion.30
  16.8 6.5 copy.21
  23.4 24.5 %convolution_convert_fusion.1 = bf16[2048,4096]{1,0:T(8,128)(2,1)} fusion(bf16[2,4096,1024]{2,1,0:T(8,128)(2,1)} %param.15, bf16[1,2048,1024]{2,1,0:T(8,128)(2,1)} %param.12), kind=kOutput, calls=%fused_computation.55 | convolution fusion | flops 17188257792 | bytes 29360128 | tf_op jit(solution)/shard_map/transpose(jvp())/dot_general | solution.py:10
  47.9 23.6 %fusion.50 = f32[2048,4096]{1,0:T(8,128)} fusion(bf16[2,1024,4096]{2,1,0:T(8,128)(2,1)} %param.13, bf16[1,2048,1024]{2,1,0:T(8,128)(2,1)S(1)} %copy-done.4, f32[2048]{0:T(1024)S(1)} %add_rsqrt_fusion), kind=kOutput, calls=%fused_computation.83 | convolution fusion | flops 17186160640 | bytes 46145536 | tf_op jit(solution)/shard_map/dot_general | solution.py:21
  71.5 38.6 %multiply_convert_fusion.1 = (bf16[2048,4096]{1,0:T(8,128)(2,1)}, f32[2048,4096]{1,0:T(8,128)}) fusion(f32[2048,4096]{1,0:T(8,128)} %fusion.50, bf16[2,1024,4096]{2,1,0:T(8,128)(2,1)} %param.14, bf16[1,2048,1024]{2,1,0:T(8,128)(2,1)} %param.11, f32[2048]{0:T(1024)S(1)} %add_rsqrt_fusion), kind=kOutput, calls=%fused_computation.44 | convolution fusion | flops 17236492288 | bytes 96477184 | tf_op jit(solution)/shard_map/dot_general | solution.py:22
  110.0 23.5 %fusion.34 = (f32[2048]{0:T(1024)S(1)}, bf16[2048,1024]{0,1:T(8,128)(2,1)S(1)}) fusion(bf16[2048,4096]{1,0:T(8,128)(2,1)} %get-tuple-element.24, bf16[2,4096,1024]{2,1,0:T(8,128)(2,1)} %param.15, bf16[1,2048,1024]{1,2,0:T(8,128)(2,1)} %copy.20), kind=kOutput, calls=%fused_computation.67 | convolution fusion | flops 17190352896 | bytes 33562624 | tf_op jit(solution)/shard_map/dot_general | solution.py:10
  133.6 0.6 copy-done.5
  134.2 1.4 copy-done.2
  135.6 23.6 %fusion.37 = f32[2048,4096]{1,0:T(8,128)} fusion(bf16[2,1024,4096]{2,1,0:T(8,128)(2,1)} %param.14, bf16[2048,1024]{0,1:T(8,128)(2,1)S(1)} %get-tuple-element.27, f32[2048]{0:T(1024)S(1)} %fusion.80), kind=kOutput, calls=%fused_computation.70 | convolution fusion | flops 17186160640 | bytes 46145536 | tf_op jit(solution)/shard_map/jvp()/dot_general | solution.py:22
  159.2 46.6 %fusion.14 = (bf16[2048,4096]{1,0:T(8,128)(2,1)}, f32[2048,4096]{1,0:T(8,128)}) fusion(f32[2048,4096]{1,0:T(8,128)} %fusion.37, bf16[2048,4096]{1,0:T(8,128)(2,1)} %convolution_convert_fusion.1, bf16[2,1024,4096]{2,1,0:T(8,128)(2,1)} %param.13, bf16[2048,1024]{0,1:T(8,128)(2,1)} %copy-done.2, f32[2048]{0:T(1024)S(1)} %fusion.80), kind=kOutput, calls=%fused_computation.32 | convolution fusion | flops 17286823936 | bytes 113254400 | tf_op jit(solution)/shard_map/jvp()/dot_general | solution.py:21
  205.7 27.1 %fusion.27 = bf16[2048,1024]{0,1:T(8,128)(2,1)} fusion(bf16[2048,4096]{1,0:T(8,128)(2,1)} %convolution_convert_fusion.1, bf16[2,1024,4096]{2,1,0:T(8,128)(2,1)} %param.14, f32[2048,4096]{1,0:T(8,128)} %get-tuple-element.29), kind=kOutput, calls=%fused_computation.48 | convolution fusion | flops 17230200832 | bytes 62914560 | tf_op jit(solution)/shard_map/transpose(jvp())/dot_general | solution.py:22
  232.9 26.7 %convert_bitcast_fusion.2 = bf16[1,1024,4096]{2,1,0:T(8,128)(2,1)} fusion(bf16[2048,4096]{1,0:T(8,128)(2,1)} %convolution_convert_fusion.1, bf16[2048,1024]{0,1:T(8,128)(2,1)} %copy-done.2, f32[2048]{0:T(1024)S(1)} %fusion.80, f32[2048,4096]{1,0:T(8,128)} %get-tuple-element.29), kind=kOutput, calls=%fused_computation.87 | convolution fusion | flops 17240686592 | bytes 62922752 | tf_op jit(solution)/shard_map/transpose(jvp())/dot_general | solution.py:22
  259.5 30.9 %convert_bitcast_fusion = bf16[1,4096,1024]{2,1,0:T(8,128)(2,1)} fusion(f32[2048,4096]{1,0:T(8,128)} %fusion.37, bf16[1,2048,1024]{2,1,0:T(8,128)(2,1)} %param.12, f32[2048,4096]{1,0:T(8,128)} %get-tuple-element.29), kind=kOutput, calls=%fused_computation.85 | convolution fusion | flops 17234395136 | bytes 79691776 | tf_op jit(solution)/shard_map/transpose(jvp())/dot_general | solution.py:10
  290.5 21.6 %convert_bitcast_fusion.4 = bf16[1,1024,4096]{2,1,0:T(8,128)(2,1)} fusion(bf16[2048,4096]{1,0:T(8,128)(2,1)} %get-tuple-element.28, bf16[2048,1024]{0,1:T(8,128)(2,1)S(1)} %copy-done.3, f32[2048]{0:T(1024)S(1)} %fusion.80), kind=kOutput, calls=%fused_computation.89 | convolution fusion | flops 17186160640 | bytes 29368320 | tf_op jit(solution)/shard_map/transpose(jvp())/dot_general | solution.py:21
  312.1 25.4 %fusion.36 = (f32[2048]{0:T(1024)S(1)}, bf16[2048,1024]{0,1:T(8,128)(2,1)}) fusion(bf16[2048,1024]{0,1:T(8,128)(2,1)S(1)} %copy-done.3, bf16[2048,1024]{0,1:T(8,128)(2,1)} %fusion.27, bf16[2048,4096]{1,0:T(8,128)(2,1)} %get-tuple-element.28, bf16[2,1024,4096]{2,1,0:T(8,128)(2,1)} %param.13), kind=kOutput, calls=%fused_computation.69 | convolution fusion | flops 17190352896 | bytes 37756928 | tf_op jit(solution)/shard_map/transpose(jvp())/dot_general | solution.py:21
  337.5 6.0 fusion.65
  343.5 25.0 %convolution_convert_fusion = bf16[2048,4096]{1,0:T(8,128)(2,1)} fusion(bf16[2048,1024]{0,1:T(8,128)(2,1)} %fusion.65, bf16[2,4096,1024]{2,1,0:T(8,128)(2,1)} %param.15), kind=kOutput, calls=%fused_computation.54 | convolution fusion | flops 17188257792 | bytes 29360128 | tf_op jit(solution)/shard_map/transpose(jvp())/dot_general | solution.py:10
  368.5 24.4 %convert_bitcast_fusion.1 = bf16[1,4096,1024]{2,1,0:T(8,128)(2,1)} fusion(bf16[2048,4096]{1,0:T(8,128)(2,1)} %get-tuple-element.24, bf16[2048,1024]{0,1:T(8,128)(2,1)} %fusion.65), kind=kOutput, calls=%fused_computation.86 | convolution fusion | flops 17184063488 | bytes 29360128 | tf_op jit(solution)/shard_map/transpose(jvp())/dot_general | solution.py:10
  392.9 25.5 %convert_bitcast_fusion.3 = bf16[1,1024,4096]{2,1,0:T(8,128)(2,1)} fusion(bf16[2048,4096]{1,0:T(8,128)(2,1)} %convolution_convert_fusion, f32[2048,4096]{1,0:T(8,128)} %fusion.50, bf16[1,2048,1024]{1,2,0:T(8,128)(2,1)S(1)} %copy-done.1, f32[2048]{0:T(1024)S(1)} %copy-done.8), kind=kOutput, calls=%fused_computation.88 | convolution fusion | flops 17240686592 | bytes 62922752 | tf_op jit(solution)/shard_map/transpose(jvp())/dot_general | solution.py:22
  418.5 37.1 %convert_bitcast_fusion.5 = bf16[1,1024,4096]{2,1,0:T(8,128)(2,1)} fusion(f32[2048,4096]{1,0:T(8,128)} %fusion.50, f32[2048,4096]{1,0:T(8,128)} %get-tuple-element.25, bf16[2048,4096]{1,0:T(8,128)(2,1)} %convolution_convert_fusion, bf16[1,2048,1024]{1,2,0:T(8,128)(2,1)} %copy.20, f32[2048]{0:T(1024)S(1)} %copy-done.8), kind=kOutput, calls=%fused_computation.90 | convolution fusion | flops 17282629632 | bytes 96477184 | tf_op jit(solution)/shard_map/transpose(jvp())/dot_general | solution.py:21
  455.5 570.2 %all-reduce.3.cloned.1.call-done = (bf16[1,1024,4096]{2,1,0:T(8,128)(2,1)}, bf16[1,1024,4096]{2,1,0:T(8,128)(2,1)}, bf16[1,1024,4096]{2,1,0:T(8,128)(2,1)}, bf16...) async-done(((bf16[1,1024,4096]{2,1,0:T(8,128)(2,1)}, bf16[1,1024,4096]{2,1,0:T(8,128)(2,1)}, ...) | async-done | bytes 50331664 | tf_op jit(solution)/shard_map/psum | solution.py:45
  1025.8 57.5 %fusion.11 = (bf16[2,4096,1024]{2,1,0:T(8,128)(2,1)}, f32[2,4096,1024]{2,1,0:T(8,128)}, f32[2,4096,1024]{2,1,0:T(8,128)}) fusion(bf16[2,4096,1024]{2,1,0:T(8,128)(2,1)} %param.15, bf16[1,4096,1024]{2,1,0:T(8,128)(2,1)} %get-tuple-element.13, bf16[1,4096,1024]{2,1,0:T(8,128)(2,1)} %get-tuple-element.14, f32[2,4096,1024]{2,1,0:T(8,128)} %param.21, ...), kind=kLoop, calls=%fused_computation.29 | loop fusion | flops 159383552 | bytes 184549376 | tf_op jit(solution)/shard_map/convert_element_type | solution.py:30
  1083.3 116.2 %fusion.2 = (bf16[2,1024,4096]{2,1,0:T(8,128)(2,1)}, f32[2,1024,4096]{2,1,0:T(8,128)}, f32[2,1024,4096]{2,1,0:T(8,128)}, bf16[2,1024,4096]{2,1,0:T(8,128)(2,1)},...) fusion(bf16[2,1024,4096]{2,1,0:T(8,128)(2,1)} %param.13, bf16[1,1024,4096]{2,1,0:T(8,128)(2,1)} %get-tuple-element.9, ...), kind=kLoop, calls=%fused_computation.20 | loop fusion | flops 318767104 | bytes 369098752 | tf_op jit(solution)/shard_map/convert_element_type | solution.py:30
  (21 shorter events, 0.1 us)
Async XLA Ops:
  7.2 1018.6 %all-reduce.3.cloned.1.call-start = ((), (), s32[]{:S(2)}) async-start(), calls=%async_computation | async-start | bytes 100663296 | tf_op jit(solution)/shard_map/psum | solution.py:45
  16.8 54.6 %copy-start.7 = (f32[2048]{0:T(1024)}, f32[2048]{0:T(1024)S(1)}, u32[]{:S(2)}) copy-start(f32[2048]{0:T(1024)S(1)} %add_rsqrt_fusion) | copy-start | bytes 24580
  23.4 24.5 %copy-start.4 = (bf16[1,2048,1024]{2,1,0:T(8,128)(2,1)S(1)}, bf16[1,2048,1024]{2,1,0:T(8,128)(2,1)}, u32[]{:S(2)}) copy-start(bf16[1,2048,1024]{2,1,0:T(8,128)(2,1)} %param.11) | copy-start | bytes 12582916
  133.6 0.6 copy-start.5
  133.6 2.0 copy-start.2
  259.5 30.9 %copy-start.3 = (bf16[2048,1024]{0,1:T(8,128)(2,1)S(1)}, bf16[2048,1024]{0,1:T(8,128)(2,1)}, u32[]{:S(2)}) copy-start(bf16[2048,1024]{0,1:T(8,128)(2,1)} %copy-done.2) | copy-start | bytes 12582916
  312.1 25.4 %copy-start.6 = (f32[2048]{0:T(1024)S(1)}, f32[2048]{0:T(1024)}, u32[]{:S(2)}) copy-start(f32[2048]{0:T(1024)} %copy-done.5) | copy-start | bytes 24580
  312.1 25.4 %copy-start = (bf16[1,2048,1024]{1,2,0:T(8,128)(2,1)S(1)}, bf16[1,2048,1024]{1,2,0:T(8,128)(2,1)}, u32[]{:S(2)}) copy-start(bf16[1,2048,1024]{1,2,0:T(8,128)(2,1)} %copy.21) | copy-start | bytes 12582916
  368.5 24.4 %copy-start.1 = (bf16[1,2048,1024]{1,2,0:T(8,128)(2,1)S(1)}, bf16[1,2048,1024]{1,2,0:T(8,128)(2,1)}, u32[]{:S(2)}) copy-start(bf16[1,2048,1024]{1,2,0:T(8,128)(2,1)} %copy.20) | copy-start | bytes 12582916
  368.5 24.4 %copy-start.8 = (f32[2048]{0:T(1024)S(1)}, f32[2048]{0:T(1024)}, u32[]{:S(2)}) copy-start(f32[2048]{0:T(1024)} %copy-done.7) | copy-start | bytes 24580
Sparse Core Ops, SparseCore 0:
  455.7 570.0 all-reduce.2
where the time goes:
time: 1210 us
  waiting for transfers between devices  570 us (47%)
  matrix products  424 us (35%)
  other arithmetic  183 us (15%)
  local copies, waits for them, and re-layouts  15 us (1%)
  between operations  14.5 us (1%)
    psum x1, waiting for transfers between devices, step(): summed[number] = [lax.psum(by_w[name], 'dp') for name in NAMES]  570 us
    convert_element_type x2, other arithmetic, adamw(): return ((w - 0.02 * step).astype(jnp.bfloat16), m, v)  174 us
    dot_general x5, matrix products, layer(): gate = jnp.dot(a, w['w_gate'], preferred_element_type=jnp.float32)  154 us
    dot_general x5, matrix products, layer(): up = jnp.dot(a, w['w_up'], preferred_element_type=jnp.float32)  142 us
    dot_general x5, matrix products, matmul(): jnp.dot(a, w, preferred_element_type=jnp.float32).astype(jnp.bfloat16)  128 us
  transfers between devices with their start and end apart: 1, of which 1 were waited for; matrix products, arithmetic and copies ran while one was open for 0% of the time, Pallas kernels for 0%

commit v1 on v0

v1 whole, which is shorter than its diff:
```python
import functools

import jax
import jax.numpy as jnp
from jax import lax
from jax.experimental import pallas as pl
from jax.experimental.pallas import tpu as pltpu
from jax.sharding import PartitionSpec as P

F32, BF16 = jnp.float32, jnp.bfloat16
MESH = pl.DeviceIdType.MESH
H = 512
TB = 512
RING = 3
GROUPS = (8, 5, 3)


def dot(a, b, ca=1, cb=0):
    return lax.dot_general(a, b, (((ca,), (cb,)), ((), ())), preferred_element_type=F32)


def ds(i, n):
    return pl.ds(pl.multiple_of(i * n, n), n)


def step_kernel(
    x, dy, wg, wu, wd, shard, pq, acts, h1, a0t,
    a, at, c, ct, acc, wgu_v, wd_v, r0, r1, r2, k1, s1, k2, s2, sv, w_sem, in_sem, pq_sem, act_sem, sv_sem,
    send0, recv0, send1, recv1, send2, recv2, free0, free1, free2,
):
    tokens, d = x.shape
    ff = wd.shape[1]
    nc = ff // H
    nb = tokens // TB
    total = 2 * nc
    me = lax.axis_index("dp")
    mc, my, mx = me % 2, (me // 2) % 2, me // 4
    over_c, over_y, over_x = me + 1 - 2 * mc, me + 2 - 4 * my, me + 4 - 8 * mx
    barrier = pltpu.get_barrier_semaphore()
    for peer in (over_c, over_y, over_x):
        pl.semaphore_signal(barrier, inc=1, device_id={"dp": peer}, device_id_type=MESH)

    def weights(n):
        j, slot = n % nc, n % 2
        lay = jnp.where((n >= nc) & (n < 2 * nc), 1, 0)
        return (
            pltpu.make_async_copy(wd.at[lay, ds(j, H), :], wd_v.at[slot], w_sem.at[slot, 0]),
            pltpu.make_async_copy(wg.at[lay, :, ds(j, H)], wgu_v.at[slot, :, pl.ds(0, H)], w_sem.at[slot, 1]),
            pltpu.make_async_copy(wu.at[lay, :, ds(j, H)], wgu_v.at[slot, :, pl.ds(H, H)], w_sem.at[slot, 2]),
        )

    def pq_load(j, tb):
        return pltpu.make_async_copy(pq.at[j, ds(tb, TB), :], acc.at[ds(tb, TB), :], pq_sem.at[tb])

    def copy0(s, dwb):
        return pltpu.make_async_remote_copy(
            dwb.at[s % 2, :, 1 - mc], r0.at[s % 2], send0.at[s % 2], recv0.at[s], device_id={"dp": over_c}, device_id_type=MESH
        )

    def copy1(s, ab):
        return pltpu.make_async_remote_copy(
            s1.at[s % 2, ab], r1.at[s % RING, ab], send1.at[s % 2, ab], recv1.at[s, ab],
            device_id={"dp": (over_x, over_y)[ab]}, device_id_type=MESH,
        )

    def copy2(s, ab):
        return pltpu.make_async_remote_copy(
            s2.at[s % 2, ab], r2.at[s % RING, ab], send2.at[s % 2, ab], recv2.at[s, ab],
            device_id={"dp": (over_y, over_x)[ab]}, device_id_type=MESH,
        )

    def out_copy(s):
        return pltpu.make_async_copy(sv.at[s % 2], shard.at[s], sv_sem.at[s % 2])

    def send_own(s, dwb):
        @pl.when(s >= 2)
        def _():
            pl.semaphore_wait(free0, 1)

        copy0(s, dwb).start()

    def reduce1(s, dwb):
        copy0(s, dwb).wait()

        @pl.when(s >= 2)
        def _():
            for ab in range(2):
                copy1(s - 2, ab).wait_send()

        slot = s % 2

        def one(i, _):
            k, o = i // 2, i % 2
            for ab in range(2):
                rows = pl.ds(ab * 64, 64)
                keep = k * 4 + (mx * 2 + o if ab == 0 else o * 2 + my)
                give = k * 4 + ((1 - mx) * 2 + o if ab == 0 else o * 2 + 1 - my)
                k1[slot, ab, i] = dwb[slot, keep, mc, rows, :].astype(F32) + r0[slot, keep, rows, :].astype(F32)
                s1[slot, ab, i] = (dwb[slot, give, mc, rows, :].astype(F32) + r0[slot, give, rows, :].astype(F32)).astype(BF16)
            return 0

        lax.fori_loop(0, 6, one, 0)

        @pl.when(s + 2 < total)
        def _():
            pl.semaphore_signal(free0, inc=1, device_id={"dp": over_c}, device_id_type=MESH)

        @pl.when(s >= RING)
        def _():
            for ab in range(2):
                pl.semaphore_wait(free1.at[ab], 1)

        for ab in range(2):
            copy1(s, ab).start()

    def reduce2(s):
        slot, ring = s % 2, s % RING

        @pl.when(s >= 2)
        def _():
            for ab in range(2):
                copy2(s - 2, ab).wait_send()

        for ab in range(2):
            copy1(s, ab).wait_recv()

        def one(k, _):
            for ab in range(2):
                mine = (my, mx)[ab]
                keep, give = k * 2 + mine, k * 2 + 1 - mine
                k2[slot, ab, k] = k1[slot, ab, keep] + r1[ring, ab, keep].astype(F32)
                s2[slot, ab, k] = (k1[slot, ab, give] + r1[ring, ab, give].astype(F32)).astype(BF16)
            return 0

        lax.fori_loop(0, 3, one, 0)

        @pl.when(s + RING < total)
        def _():
            for ab in range(2):
                pl.semaphore_signal(free1.at[ab], inc=1, device_id={"dp": (over_x, over_y)[ab]}, device_id_type=MESH)

        @pl.when(s >= RING)
        def _():
            for ab in range(2):
                pl.semaphore_wait(free2.at[ab], 1)

        for ab in range(2):
            copy2(s, ab).start()

    def reduce3(s):
        slot, ring = s % 2, s % RING

        @pl.when(s >= 2)
        def _():
            out_copy(s - 2).wait()

        for ab in range(2):
            copy2(s, ab).wait_recv()

        def one(k, _):
            for ab in range(2):
                sv[slot, k, pl.ds(ab * 64, 64), :] = (k2[slot, ab, k] + r2[ring, ab, k].astype(F32)).astype(BF16)
            return 0

        lax.fori_loop(0, 3, one, 0)

        @pl.when(s + RING < total)
        def _():
            for ab in range(2):
                pl.semaphore_signal(free2.at[ab], inc=1, device_id={"dp": (over_y, over_x)[ab]}, device_id_type=MESH)

        out_copy(s).start()

    def when(cond, f, *args):
        @pl.when(cond)
        def _():
            f(*args)

    for w in weights(0):
        w.start()

    def forward(xb, stage, stage_act):
        loads = [pltpu.make_async_copy(x.at[ds(tb, TB), :], xb.at[ds(tb, TB), :], in_sem.at[tb]) for tb in range(nb)]
        dy_load = pltpu.make_async_copy(dy, c, in_sem.at[nb])
        for load in loads:
            load.start()
        dy_load.start()
        for load in loads:
            load.wait()

        def norm(tb, _):
            r = ds(tb, 256)
            wide = xb[r, :].astype(F32)
            scale = lax.rsqrt(jnp.mean(wide * wide, -1, keepdims=True) + 1e-6)
            a[r, :] = (wide * scale).astype(BF16)
            acc[r, :] = jnp.zeros((256, d), F32)
            return 0

        lax.fori_loop(0, tokens // 256, norm, 0)
        dy_load.wait()

        def stored(n):
            j, tb = n // nb, n % nb
            return (
                pltpu.make_async_copy(stage.at[n % 2], pq.at[j, ds(tb, TB), :], pq_sem.at[n % 2]),
                pltpu.make_async_copy(stage_act.at[n % 2], acts.at[j, ds(tb, TB), :], act_sem.at[n % 2]),
            )

        def chunk(j, _):
            slot = j % 2
            for w in weights(j + 1):
                w.start()
            for w in weights(j):
                w.wait()

            def block(tb, _):
                n = j * nb + tb
                r = ds(tb, TB)

                @pl.when(n >= 2)
                def _():
                    for store in stored(n - 2):
                        store.wait()

                gu = dot(a[r, :], wgu_v[slot])
                g, u = gu[:, :H], gu[:, H:]
                s = jax.nn.sigmoid(g)
                p = g * s
                act = (p * u).astype(BF16)
                stage[n % 2, :, :H] = p
                stage[n % 2, :, H:] = u * (s + p * (1 - s))
                stage_act[n % 2] = act
                acc[r, :] += dot(act, wd_v[slot])
                tr, tc = ds(n // 2, 128), ds(n % 2, d // 2)
                ct[tc, tr] = c[tr, tc].T
                at[tc, tr] = a[tr, tc].T
                for store in stored(n):
                    store.start()
                return 0

            lax.fori_loop(0, nb, block, 0)
            return 0

        lax.fori_loop(0, nc, chunk, 0)
        last = nc * nb
        for n in (last - 2, last - 1):
            for store in stored(n):
                store.wait()
        keep_at = pltpu.make_async_copy(at, a0t, in_sem.at[nb])
        keep_at.start()

        def finish(tb, _):
            r = ds(tb, 256)
            xb[r, :] = (xb[r, :].astype(F32) + acc[r, :].astype(BF16).astype(F32)).astype(BF16)
            wide = xb[r, :].astype(F32)
            scale = lax.rsqrt(jnp.mean(wide * wide, -1, keepdims=True) + 1e-6)
            a[r, :] = (wide * scale).astype(BF16)
            acc[r, :] = jnp.zeros((256, d), F32)
            return 0

        lax.fori_loop(0, tokens // 256, finish, 0)
        keep_h = pltpu.make_async_copy(xb, h1, in_sem.at[0])
        keep_h.start()
        keep_at.wait()

        def turn(tb, _):
            r = ds(tb, 256)
            at[:, r] = a[r, :].T
            return 0

        lax.fori_loop(0, tokens // 256, turn, 0)
        keep_h.wait()

    pl.run_scoped(
        forward, pltpu.VMEM((tokens, d), BF16), pltpu.VMEM((2, TB, 2 * H), F32), pltpu.VMEM((2, TB, H), BF16)
    )
    pl.semaphore_wait(barrier, 3)

    def backward(act, dgu, dwb):
        def gradients(s):
            slot = s % 2

            def half(xh, _):
                rows = ds(xh, d // 2)
                both = dot(at[rows, :], dgu[...]).astype(BF16)
                down = dot(ct[rows, :], act[...]).astype(BF16)
                for k, part in enumerate((both[:, :H], both[:, H:], down)):
                    for y in range(2):
                        for core in range(2):
                            dwb[slot, k * 4 + xh * 2 + y, core] = part[(y * 2 + core) * 128 : (y * 2 + core + 1) * 128]
                return 0

            lax.fori_loop(0, 2, half, 0)

        def chunk1(s, _):
            n = nc + s
            slot = n % 2
            for w in weights(n + 1):
                w.start()
            for w in weights(n):
                w.wait()

            def block(tb, _):
                r = ds(tb, TB)
                gu = dot(a[r, :], wgu_v[slot])
                dact = dot(c[r, :], wd_v[slot], 1, 1).astype(BF16).astype(F32)
                g, u = gu[:, :H], gu[:, H:]
                sg = jax.nn.sigmoid(g)
                p = g * sg
                act[r, :] = (p * u).astype(BF16)
                dgu[r, H:] = (dact * p).astype(BF16)
                dgu[r, :H] = (dact * (u * (sg + p * (1 - sg)))).astype(BF16)
                return 0

            lax.fori_loop(0, nb, block, 0)
            when(s == nc - 1, lambda: pltpu.make_async_copy(h1, a, in_sem.at[0]).start())
            when(s >= 2, reduce3, s - 2)
            gradients(s)
            send_own(s, dwb)
            when(s >= 1, reduce2, s - 1)

            def back(tb, _):
                r = ds(tb, TB)
                acc[r, :] += dot(dgu[r, :], wgu_v[slot], 1, 1)
                return 0

            lax.fori_loop(0, nb, back, 0)
            reduce1(s, dwb)
            return 0

        lax.fori_loop(0, nc, chunk1, 0)

        load_at = pltpu.make_async_copy(a0t, at, in_sem.at[1])
        load_at.start()
        pltpu.make_async_copy(h1, a, in_sem.at[0]).wait()

        def act_load(j):
            return pltpu.make_async_copy(acts.at[j], act, act_sem.at[0])

        act_load(0).start()
        for tb in range(nb):

            def norm_back(i, _):
                r = pl.ds(pl.multiple_of(tb * TB + i * 256, 256), 256)
                wide = a[r, :].astype(F32)
                scale = lax.rsqrt(jnp.mean(wide * wide, -1, keepdims=True) + 1e-6)
                da = acc[r, :].astype(BF16).astype(F32)
                inner = jnp.mean(da * wide, -1, keepdims=True)
                dh = (da * scale - wide * (inner * scale * scale * scale)).astype(BF16).astype(F32)
                dh = (c[r, :].astype(F32) + dh).astype(BF16)
                c[r, :] = dh
                ct[:, r] = dh.T
                return 0

            lax.fori_loop(0, TB // 256, norm_back, 0)
            pq_load(0, tb).start()
        load_at.wait()

        def chunk0(s, _):
            n = nc + s
            j, slot = s - nc, n % 2

            @pl.when(j + 1 < nc)
            def _():
                weights(n + 1)[0].start()

            weights(n)[0].wait()

            @pl.when(j == 0)
            def _():
                for w in weights(2 * nc)[1:]:
                    w.wait()

            def block(tb, _):
                r = ds(tb, TB)
                pq_load(j, tb).wait()
                dact = dot(c[r, :], wd_v[slot], 1, 1).astype(BF16).astype(F32)
                dgu[r, H:] = (dact * acc[r, :H]).astype(BF16)
                dgu[r, :H] = (dact * acc[r, H:]).astype(BF16)
                when(j + 1 < nc, lambda: pq_load(j + 1, tb).start())
                return 0

            lax.fori_loop(0, nb, block, 0)
            when(j >= 1, reduce1, s - 1, dwb)
            act_load(j).wait()
            gradients(s)
            when(j + 1 < nc, lambda: act_load(j + 1).start())
            send_own(s, dwb)

            @pl.when(j >= 1)
            def _():
                reduce2(s - 2)
                reduce3(s - 3)

            return 0

        lax.fori_loop(nc, 2 * nc, chunk0, 0)

        end = total - 1
        reduce1(end, dwb)
        reduce2(end - 1)
        reduce3(end - 2)
        reduce2(end)
        reduce3(end - 1)
        reduce3(end)
        for s in (end - 1, end):
            out_copy(s).wait()
            for ab in range(2):
                copy1(s, ab).wait_send()
                copy2(s, ab).wait_send()

    pl.run_scoped(
        backward,
        pltpu.VMEM((tokens, H), BF16),
        pltpu.VMEM((tokens, 2 * H), BF16),
        pltpu.VMEM((2, 12, 2, 128, H), BF16),
    )


def gradients_of(x, dy, wg, wu, wd):
    tokens, d = x.shape
    ff = wd.shape[1]
    nc, nb = ff // H, tokens // TB
    any_, vmem, dma = pl.BlockSpec(memory_space=pl.ANY), pltpu.VMEM, pltpu.SemaphoreType.DMA
    shapes = [
        ((2 * nc, 3, d // 8, H), BF16),
        ((nc, tokens, 2 * H), F32),
        ((nc, tokens, H), BF16),
        ((tokens, d), BF16),
        ((d, tokens), BF16),
    ]
    flops = 30 * tokens * d * ff
    return pl.pallas_call(
        step_kernel,
        name="train_step",
        out_shape=[jax.ShapeDtypeStruct(*one) for one in shapes],
        in_specs=[any_] * 5,
        out_specs=[any_] * 5,
        scratch_shapes=[
            vmem((tokens, d), BF16),
            vmem((d, tokens), BF16),
            vmem((tokens, d), BF16),
            vmem((d, tokens), BF16),
            vmem((tokens, d), F32),
            vmem((2, d, 2 * H), BF16),
            vmem((2, H, d), BF16),
            vmem((2, 12, 128, H), BF16),
            vmem((RING, 2, 6, 64, H), BF16),
            vmem((RING, 2, 3, 64, H), BF16),
            vmem((2, 2, 6, 64, H), F32),
            vmem((2, 2, 6, 64, H), BF16),
            vmem((2, 2, 3, 64, H), F32),
            vmem((2, 2, 3, 64, H), BF16),
            vmem((2, 3, 128, H), BF16),
            dma((2, 3)),
            dma((nb + 1,)),
            dma((nb,)),
            dma((2,)),
            dma((2,)),
            dma((2,)),
            dma((2 * nc,)),
            dma((2, 2)),
            dma((2 * nc, 2)),
            dma((2, 2)),
            dma((2 * nc, 2)),
            pltpu.SemaphoreType.REGULAR,
            pltpu.SemaphoreType.REGULAR((2,)),
            pltpu.SemaphoreType.REGULAR((2,)),
        ],
        compiler_params=pltpu.CompilerParams(collective_id=0, has_side_effects=True, vmem_limit_bytes=67_000_000),
        cost_estimate=pl.CostEstimate(flops=flops, bytes_accessed=300_000_000, transcendentals=0),
    )(x, dy, wg, wu, wd)[0]


def adam_kernel(gg, gu, gd, *refs):
    ins, outs = refs[:9], refs[-9:]
    rows = ins[0].shape[1]
    grads = (
        gg[...].reshape(rows, H),
        gu[...].reshape(rows, H),
        gd[...].reshape(gd.shape[0] * gd.shape[3], gd.shape[4]).astype(F32).T,
    )
    for i, g in enumerate(grads):
        g = g.astype(F32)
        w, m, v = ins[i][0].astype(F32), ins[3 + i][0], ins[6 + i][0]
        m = 0.9 * m + 0.1 * g
        v = 0.95 * v + 0.05 * g * g
        step = m * lax.rsqrt(v + 1e-8) + 0.1 * w
        outs[i][0] = (w - 0.02 * step).astype(BF16)
        outs[3 + i][0] = m
        outs[6 + i][0] = v


def adam(first, count, g, arrays, so_far):
    layers, d, ff = arrays[0].shape
    nc = ff // H

    def place(i):
        s = first + i
        return layers - 1 - s // nc, s % nc

    def wide(i, r):
        lay, j = place(i)
        return lay, r, j

    def tall(i, r):
        lay, j = place(i)
        return lay, j * 2 + r, 0

    g_wide = [pl.BlockSpec((4, 1, 1, 128, H), functools.partial(lambda i, r, k: (r, i, k, 0, 0), k=k)) for k in range(2)]
    g_tall = pl.BlockSpec((8, 1, 1, 128, H // 2), lambda i, r: (0, i, 2, 0, r))
    one = [pl.BlockSpec((1, d // 2, H), wide)] * 2 + [pl.BlockSpec((1, H // 2, d), tall)]
    given = len(so_far)
    params = count * 3 * d * H
    return pl.pallas_call(
        adam_kernel,
        name="adamw",
        grid=(count, 2),
        out_shape=[jax.ShapeDtypeStruct(t.shape, t.dtype) for t in arrays],
        in_specs=g_wide + [g_tall] + one * 3 + [pl.BlockSpec(memory_space=pl.ANY)] * given,
        out_specs=one * 3,
        input_output_aliases={12 + i: i for i in range(given)},
        compiler_params=pltpu.CompilerParams(vmem_limit_bytes=60_000_000),
        cost_estimate=pl.CostEstimate(flops=12 * params, bytes_accessed=22 * params, transcendentals=params),
    )(g, g, g, *arrays, *so_far)


def solution(mesh):
    def step(x, dy, *arrays):
        shard = gradients_of(x[0], dy[0], *arrays[:3])
        gathered, first = [], 0
        for count in GROUPS:
            gathered.append((first, count, lax.all_gather(shard[first : first + count], "dp", axis=0)))
            first += count
        so_far = ()
        for first, count, g in gathered:
            so_far = tuple(adam(first, count, g, arrays, so_far))
        return so_far

    return jax.shard_map(
        step,
        mesh=mesh,
        in_specs=(P(("rep", "dp"), None, None),) * 2 + (P(None, None, None),) * 9,
        out_specs=(P("rep", None, None),) * 9,
        check_vma=False,
    )
```

time: 1210 us -> 688 us (0.57)
  Pallas kernels: 0 us -> 550 us
  waiting for transfers between devices: 570 us -> 114 us
  matrix products: 424 us -> 0 us
  other arithmetic: 183 us -> 0 us
    psum x1 -> x0, waiting for transfers between devices: 570 us -> none  [step(): summed[number] = [lax.psum(by_w[name], 'dp') for name in NAMES]]
    pallas_call x0 -> x4, Pallas kernels: none -> 550 us  [the longest x1 367 us: gradients_of(): pl.pallas_call(step_kernel, name='train_step', out_shape=[jax.ShapeDtypeS...]
    dot_general x15 -> x0, matrix products: 424 us -> none  [the longest x5 154 us: layer(): gate = jnp.dot(a, w['w_gate'], preferred_element_type=jnp.float32)]
    convert_element_type x2 -> x0, other arithmetic: 174 us -> none  [adamw(): return ((w - 0.02 * step).astype(jnp.bfloat16), m, v)]
    all_gather x0 -> x3, waiting for transfers between devices: none -> 114 us  [step(): lax.all_gather(shard[first:first + count], 'dp', axis=0)]
    unnamed x20 -> x0, local copies, waits for them, and re-layouts: 15 us -> none
  transfers between devices with their start and end apart: 1 -> 3, of which waited for: 1 -> 1; matrix products, arithmetic and copies ran while one was open for 0% -> 1% of each run, Pallas kernels for 0% -> 21%
where the time goes in v1:
time: 688 us
  Pallas kernels  550 us (80%)
  waiting for transfers between devices  114 us (17%)
  between operations  13.8 us (2%)
  local copies, waits for them, and re-layouts  9.23 us (1%)
    pallas_call x1, Pallas kernels, gradients_of(): pl.pallas_call(step_kernel, name='train_step', out_shape=[jax.ShapeDtypeS...  367 us
    pallas_call x3, Pallas kernels, adam(): pl.pallas_call(adam_kernel, name='adamw', grid=(count, 2), out_shape=[jax...  184 us
    all_gather x3, waiting for transfers between devices, step(): lax.all_gather(shard[first:first + count], 'dp', axis=0)  114 us
  transfers between devices with their start and end apart: 3, of which 1 were waited for; matrix products, arithmetic and copies ran while one was open for 1% of the time, Pallas kernels for 21%

profile of v1, /device:TPU:0, one launch (start us, length us, event | category | flops | bytes accessed | tf_op | source)
XLA Modules:
  0.0 687.9 jit_solution(5740194244915108722)
XLA Ops:
  7.2 0.0 all-gather.11.cloned.1.call-start
  7.2 366.6 %train_step.1 = (bf16[16,3,128,512]{3,2,1,0:T(8,128)(2,1)}, f32[8,2048,1024]{2,1,0:T(8,128)}, bf16[8,2048,512]{2,1,0:T(8,128)(2,1)}, bf16[2048,1024]{1,0:T(8,128)(2,1)}, bf16[1024,2048]{1,0:T(8,128)(2,1)}) custom-call(bf16[2048,1024]{1,0:T(8,128)(2,1)} %bitcast.14, bf16[2048,1024]{1,0:T(8,128)(2,1)} %bitcast.15, bf16[2,1024,4096]{2,1,0:T(8,128)(2,1)} %refs_0_.5, ...), custom_call_target="tpu_custom_call" | custom-call | flops 257698037760 | bytes 300000000 | tf_op jit(solution)/shard_map/train_step/pallas_call | solution.py:433
  373.9 3.9 slice.11
  377.7 0.0 all-gather.11.cloned.1.call-update
  377.8 0.0 all-gather.9.cloned.1.call-start
  377.8 3.0 slice.10
  380.8 0.0 all-gather.9.cloned.1.call-update
  380.8 0.0 all-gather.7.cloned.1.call-start
  380.9 2.4 slice.9
  383.3 0.0 all-gather.7.cloned.1.call-update
  383.3 114.3 %all-gather.11.cloned.1.call-done = bf16[64,3,128,512]{3,2,1,0:T(8,128)(2,1)} async-done(((bf16[8,3,128,512]{3,2,1,0:T(8,128)(2,1)}), bf16[64,3,128,512]{3,2,1,0:T(8,128)(2,1)}) %all-gather.11.cloned.1.call-update) | async-done | bytes 25165840 | tf_op jit(solution)/shard_map/all_gather | solution.py:533
  497.6 89.6 %adamw.3 = (bf16[2,1024,4096]{2,1,0:T(8,128)(2,1)}, bf16[2,1024,4096]{2,1,0:T(8,128)(2,1)}, bf16[2,4096,1024]{2,1,0:T(8,128)(2,1)}, f32[2,1024,4096]{2,1,0:T(8,1...) custom-call(bf16[8,8,3,128,512]{4,3,2,1,0:T(8,128)(2,1)} %bitcast.5,, ...), custom_call_target="tpu_custom_call" | custom-call | flops 150994944 | bytes 276824064 | tf_op jit(solution)/shard_map/adamw/pallas_call | solution.py:515
  587.2 0.0 all-gather.9.cloned.1.call-done
  587.2 58.2 %adamw.4 = (bf16[2,1024,4096]{2,1,0:T(8,128)(2,1)}, bf16[2,1024,4096]{2,1,0:T(8,128)(2,1)}, bf16[2,4096,1024]{2,1,0:T(8,128)(2,1)}, f32[2,1024,4096]{2,1,0:T(8,1...) custom-call(bf16[8,5,3,128,512]{4,3,2,1,0:T(8,128)(2,1)} %bitcast.8,, ...), custom_call_target="tpu_custom_call", output_to_operand_aliasing={{0}: (12, {}), {1}: (13, {}), {2}: (14, {}), {3}: (15, {}),... | custom-call | flops 94371840 | bytes 173015040 | tf_op jit(solution)/shard_map/adamw/pallas_call | solution.py:515
  645.4 0.0 all-gather.7.cloned.1.call-done
  645.4 35.9 %adamw.5 = (bf16[2,1024,4096]{2,1,0:T(8,128)(2,1)}, bf16[2,1024,4096]{2,1,0:T(8,128)(2,1)}, bf16[2,4096,1024]{2,1,0:T(8,128)(2,1)}, f32[2,1024,4096]{2,1,0:T(8,1...) custom-call(bf16[8,3,3,128,512]{4,3,2,1,0:T(8,128)(2,1)} %bitcast.11, ...), custom_call_target="tpu_custom_call", output_to_operand_aliasing={{0}: (12, {}), {1}: (13, {}), {2}: (14, {}), {3}: (15, {}),... | custom-call | flops 56623104 | bytes 103809024 | tf_op jit(solution)/shard_map/adamw/pallas_call | solution.py:515
Async XLA Ops:
  7.2 490.4 %all-gather.11.cloned.1.call-start = ((), (), s32[]{:S(2)}) async-start(), calls=%async_computation.2 | async-start | bytes 28311552 | tf_op jit(solution)/shard_map/all_gather | solution.py:533
  377.8 209.4 %all-gather.9.cloned.1.call-start = ((), (), s32[]{:S(2)}) async-start(), calls=%async_computation.1 | async-start | bytes 17694720 | tf_op jit(solution)/shard_map/all_gather | solution.py:533
  380.8 264.6 %all-gather.7.cloned.1.call-start = ((), (), s32[]{:S(2)}) async-start(), calls=%async_computation | async-start | bytes 10616832 | tf_op jit(solution)/shard_map/all_gather | solution.py:533
Sparse Core Ops, SparseCore 0:
  377.9 119.6 all-gather.10
  499.4 79.6 all-gather.8
  580.9 52.9 all-gather.6
